TPU v7x, 512 devices: a whole 4x4x16 slice. The times are simulated.
512 devices in a mesh: level: 16 (over z), dev: 32 (over x, y, core).
Axes of the slice: x: 4, y: 4, z: 16, core: 2. Of those that a mesh axis runs over, the one named last changes fastest.
Arguments:
- fields: float32 [16, 512, 12, 128], P('level', 'dev'), may hold values from -6 to 6
- own_src: int32 [16, 512], P('level', 'dev'), may hold values from 0 to 15
- own_weight: bfloat16 [16, 512, 128, 128], P('level', 'dev'), may hold values from 0 to 1, as said below
- send_block: int32 [16, 32, 32, 2], P('level', 'dev'), may hold values from 0 to 15
- send_target: int32 [16, 32, 32, 2], P('level', 'dev'), may hold values from 0 to 15
- send_count: int32 [16, 32, 32], P('level', 'dev'), may hold values from 0 to 2, as said below
- send_weight: bfloat16 [16, 32, 32, 2, 128, 128], P('level', 'dev'), may hold values from 0 to 1, as said below
- left_block: int32 [16, 32, 16, 2], P('level', 'dev'), may hold values from 0 to 15
- left_target: int32 [16, 32, 16, 2], P('level', 'dev'), may hold values from 0 to 15
- left_count: int32 [16, 32, 16], P('level', 'dev'), may hold values from 0 to 2, as said below
- left_weight: bfloat16 [16, 32, 16, 2, 128, 128], P('level', 'dev'), may hold values from 0 to 1, as said below
Outputs:
- remapped: float32 [16, 512, 12, 128], P('level', 'dev')
- totals: float32 [12], replicated
Inputs may be any that keep to these rules, and one draw needn't show every extreme that they name: send_count[l, s, s] = 0; for every level some receiver device gets 2 live slots from every other device of the level. left_count[m, q, m] = 0; for every device index some receiver level gets 2 live slots from every other level. `own_weight`: nonnegative; entry [k, i] is zero where old cell k and new cell i differ by more than 3; each column sums to a positive intersect fraction of at most 1. `send_weight`: nonnegative; entry [k, i] is zero where old cell k and new cell i differ by more than 3; each column sums to a positive intersect fraction of at most 1. `left_weight`: nonnegative; entry [k, i] is zero where old cell k and new cell i differ by more than 3; each column sums to a positive intersect fraction of at most 1.
All inputs are finite; a program needn't handle non-finite values.
Results may differ from a plain program's by a relative error of at most 0.0045.
Values may be sent and summed in bfloat16 or wider, within the bound.
A program may use at most 64 MiB of HBM per device.

v0:
```python
import functools

import jax
import jax.numpy as jnp
from jax import lax
from jax.experimental import pallas as pl
from jax.experimental.pallas import tpu as pltpu
from jax.sharding import PartitionSpec as P

MESH = pl.DeviceIdType.MESH
F32 = jnp.float32
BF16 = jnp.bfloat16


def kernel(
    nd,
    nl,
    direct,
    own_src_hbm,
    send_block_hbm,
    send_target_hbm,
    send_count_hbm,
    left_block_hbm,
    left_target_hbm,
    left_count_hbm,
    fields_hbm,
    own_hbm,
    send_hbm,
    left_hbm,
    out_ref,
    tot_ref,
    own_src,
    send_block,
    send_target,
    send_count,
    left_block,
    left_target,
    left_count,
    fields,
    own_w,
    send_w,
    left_w,
    load_sem,
    sbuf,
    rbuf,
    s_sem,
    r_sem,
    lsbuf,
    lrbuf,
    ls_sem,
    lr_sem,
    tbuf,
    trecv,
    ts_sem,
    tr_sem,
    ubuf,
    urecv,
    us_sem,
    ur_sem,
):
    dev = lax.axis_index("dev")
    lvl = lax.axis_index("level")
    blocks, cells = own_w.shape[:2]
    comp = fields.shape[0] // blocks
    cap = send_w.shape[1]
    lcap = left_w.shape[1]
    rows = sbuf.shape[1] // cap

    barrier = pltpu.get_barrier_semaphore()
    left_peers = [lax.rem(lvl + r, nl) for r in range(1, nl)]
    send_peers = [lax.rem(dev + r, nd) for r in range(1, nd)]
    pairs = (
        (left_block_hbm, left_block),
        (left_target_hbm, left_target),
        (left_count_hbm, left_count),
        (fields_hbm, fields),
        *[(left_hbm.at[p], left_w.at[p]) for p in left_peers],
        (send_block_hbm, send_block),
        (send_target_hbm, send_target),
        (send_count_hbm, send_count),
        *[(send_hbm.at[p], send_w.at[p]) for p in send_peers],
        (own_src_hbm, own_src),
        (own_hbm, own_w),
    )
    loads = [
        pltpu.make_async_copy(src, dst, load_sem.at[i]) for i, (src, dst) in enumerate(pairs)
    ]
    for load in loads:
        load.start()

    def peer_of(l, r):
        return {"level": lax.rem(lvl + l, nl), "dev": lax.rem(dev + r, nd)}

    offsets = [
        (l, r)
        for l in reversed(range(nl))
        for r in reversed(range(nd))
        if (l or r) and (direct or not (l and r))
    ]
    for l, r in offsets:
        pl.semaphore_signal(barrier, inc=1, device_id=peer_of(l, r), device_id_type=MESH)

    part = jnp.zeros((comp, cells), F32)

    def donor(index):
        return fields[pl.ds(index, comp, stride=blocks), :]

    def product(block, weight):
        return jnp.dot(block.astype(BF16), weight, preferred_element_type=F32)

    def message(buf, r, c, slot_block, slot_target, slot_count, weights, peer):
        block = donor(slot_block[c, peer])
        block = jnp.where(c < slot_count[0, peer], block, jnp.zeros_like(block))
        term = product(block, weights[peer, c])
        target = jnp.full((rows - comp, cells), slot_target[c, peer].astype(F32), F32)
        buf[r, c * rows : (c + 1) * rows, :] = jnp.concatenate([term, target], axis=0).astype(BF16)
        return term

    first = 4 + len(left_peers)
    second = first + 3 + len(send_peers)
    for load in loads[:first]:
        load.wait()
    for r in range(1, nl):
        peer = lax.rem(lvl + r, nl)
        for c in range(lcap):
            part += message(lsbuf, r, c, left_block, left_target, left_count, left_w, peer)
    for load in loads[first:second]:
        load.wait()
    for r in range(1, nd):
        peer = lax.rem(dev + r, nd)
        for c in range(cap):
            part += message(sbuf, r, c, send_block, send_target, send_count, send_w, peer)

    for load in loads[second:]:
        load.wait()
    acc = []
    for b in range(blocks):
        term = product(donor(own_src[0, b]), own_w[b])
        part += term
        acc.append(term)

    sums = jnp.sum(part, axis=1, keepdims=True)
    same = lax.broadcasted_iota(jnp.int32, (comp, cells), 0) == lax.broadcasted_iota(
        jnp.int32, (comp, cells), 1
    )
    row = jnp.sum(jnp.where(same, sums, 0.0), axis=0, keepdims=True)
    tbuf[...] = row

    pl.semaphore_wait(barrier, len(offsets))

    sends = []

    def send(src, dst, s, d, who):
        copy = pltpu.make_async_remote_copy(
            src_ref=src, dst_ref=dst, send_sem=s, recv_sem=d, device_id=who, device_id_type=MESH
        )
        copy.start()
        sends.append(copy)
        return copy

    if direct:
        tops = [
            send(tbuf, urecv.at[i], us_sem.at[i], ur_sem.at[i], peer_of(l, r))
            for i, (l, r) in enumerate(offsets)
        ]
    else:
        tots = [
            send(tbuf, trecv.at[r], ts_sem.at[r], tr_sem.at[r], peer_of(0, r))
            for r in range(1, nd)
        ]
    lefts = [
        send(lsbuf.at[r], lrbuf.at[r], ls_sem.at[r], lr_sem.at[r], peer_of(r, 0))
        for r in range(1, nl)
    ]
    intras = [
        send(sbuf.at[r], rbuf.at[r], s_sem.at[r], r_sem.at[r], peer_of(0, r)) for r in range(1, nd)
    ]
    if not direct:
        for r, copy in enumerate(tots, 1):
            copy.wait_recv()
            row += trecv[r]
        ubuf[...] = row
        tops = [
            send(ubuf, urecv.at[i], us_sem.at[i], ur_sem.at[i], peer_of(i + 1, 0))
            for i in range(nl - 1)
        ]

    def place(buf, r, slots):
        for c in range(slots):
            got = buf[r, c * rows : (c + 1) * rows, :].astype(F32)
            term = got[:comp]
            target = jnp.broadcast_to(got[comp : comp + 1], (comp, cells))
            for b in range(blocks):
                acc[b] = acc[b] + jnp.where(target == float(b), term, 0.0)

    for r, copy in enumerate(intras, 1):
        copy.wait_recv()
        place(rbuf, r, cap)
    for r, copy in enumerate(lefts, 1):
        copy.wait_recv()
        place(lrbuf, r, lcap)
    for b in range(blocks):
        out_ref[pl.ds(b, comp, stride=blocks), :] = acc[b]
    for copy in sends:
        copy.wait_send()
    for copy in tops:
        copy.wait_recv()
    terms = [row] + [urecv[i] for i in range(len(tops))]
    while len(terms) > 1:
        half = len(terms) // 2
        terms = [a + b for a, b in zip(terms[:half], terms[half:])] + terms[2 * half :]
    row = terms[0]
    tot_ref[...] = (row / (cells * blocks))[0, :comp]


def solution(mesh):
    nd = mesh.shape["dev"]
    nl = mesh.shape["level"]
    direct = nd * nl <= 64
    last = (nd if direct else 1) * nl

    def body(
        fields,
        own_src,
        own_weight,
        send_block,
        send_target,
        send_count,
        send_weight,
        left_block,
        left_target,
        left_count,
        left_weight,
    ):
        blocks, comp, cells = fields.shape[1:]
        cap = send_weight.shape[3]
        lcap = left_weight.shape[3]
        rows = -(-(comp + 1) // 16) * 16
        smem = functools.partial(pltpu.SMEM, dtype=jnp.int32)
        hbm = pl.BlockSpec(memory_space=pl.ANY)
        vmem = pl.BlockSpec(memory_space=pltpu.VMEM)
        dma = pltpu.SemaphoreType.DMA
        remapped, totals = pl.pallas_call(
            functools.partial(kernel, nd, nl, direct),
            out_shape=(
                pltpu.VMEM((comp * blocks, cells), F32),
                pltpu.VMEM((comp,), F32),
            ),
            in_specs=[hbm] * 11,
            out_specs=(vmem, vmem),
            scratch_shapes=[
                smem((1, blocks)),
                smem((cap, nd)),
                smem((cap, nd)),
                smem((1, nd)),
                smem((lcap, nl)),
                smem((lcap, nl)),
                smem((1, nl)),
                pltpu.VMEM((comp * blocks, cells), F32),
                pltpu.VMEM((blocks, cells, cells), BF16),
                pltpu.VMEM((nd, cap, cells, cells), BF16),
                pltpu.VMEM((nl, lcap, cells, cells), BF16),
                dma((9 + nd + nl,)),
                pltpu.VMEM((nd, cap * rows, cells), BF16),
                pltpu.VMEM((nd, cap * rows, cells), BF16),
                dma((nd,)),
                dma((nd,)),
                pltpu.VMEM((nl, lcap * rows, cells), BF16),
                pltpu.VMEM((nl, lcap * rows, cells), BF16),
                dma((nl,)),
                dma((nl,)),
                pltpu.VMEM((1, cells), F32),
                pltpu.VMEM((nd, 1, cells), F32),
                dma((nd,)),
                dma((nd,)),
                pltpu.VMEM((1, cells), F32),
                pltpu.VMEM((last, 1, cells), F32),
                dma((last,)),
                dma((last,)),
            ],
            compiler_params=pltpu.CompilerParams(collective_id=0, has_side_effects=True),
        )(
            own_src,
            send_block[0, 0].T,
            send_target[0, 0].T,
            send_count[0],
            left_block[0, 0].T,
            left_target[0, 0].T,
            left_count[0],
            fields[0].transpose(1, 0, 2).reshape(comp * blocks, cells),
            own_weight[0],
            send_weight[0, 0],
            left_weight[0, 0],
        )
        remapped = remapped.reshape(comp, blocks, cells).transpose(1, 0, 2)
        return remapped[None], totals

    in_specs = (
        P("level", "dev", None, None),
        P("level", "dev"),
        P("level", "dev", None, None),
        P("level", "dev", None, None),
        P("level", "dev", None, None),
        P("level", "dev", None),
        P("level", "dev", None, None, None, None),
        P("level", "dev", None, None),
        P("level", "dev", None, None),
        P("level", "dev", None),
        P("level", "dev", None, None, None, None),
    )
    out_specs = (P("level", "dev", None, None), P())
    return jax.shard_map(body, mesh=mesh, in_specs=in_specs, out_specs=out_specs, check_vma=False)
```

profile of v0, /device:TPU:1, one launch (start us, length us, event | category | flops | bytes accessed | tf_op | source)
XLA Modules:
  0.0 31.9 jit_solution(1870695367046718898)
XLA Ops:
  0.6 30.1 %shard_map.122 = (f32[192,128]{1,0:T(8,128)S(1)}, f32[12]{0:T(128)S(1)}) custom-call(s32[1,16]{1,0:T(1,128)} %own_src_hbm.1, s32[2,32]{1,0:T(2,128)} %bitcast.32, s32[2,32]{1,0:T(2,128)} %bitcast.33, s32[1,32]{1,0:T(1,128)} %bitcast.36, s32[2,16]{1,0:T(2,128)} %bitcast.34, s32[2,16]{1,0:T(2,128)} %bitcast.35, s32[1,16]{1,0:T(1,128)} %bitcast.37, ...), custom_call_target="tpu_custom_call" | custom-call | tf_op jit(solution)/shard_map/pallas_call | solution.py:243
  30.8 0.6 %copy.15 = f32[1,16,12,128]{3,1,2,0:T(8,128)} copy(f32[1,16,12,128]{3,1,2,0:T(8,128)S(1)} %bitcast.27) | data formatting | bytes 196608
  31.4 0.5 %copy.16 = f32[12]{0:T(128)} copy(f32[12]{0:T(128)S(1)} %get-tuple-element.7) | data formatting | bytes 96
where the time goes:
time: 32.1 us; the launch traced here: 31.9 us
  Pallas kernels  30.1 us (94%)
  local copies, waits for them, and re-layouts  1.15 us (4%)
  between operations  0.64 us (2%)
    pallas_call x1, Pallas kernels, body(): pl.pallas_call(functools.partial(kernel, nd, nl, direct), out_shape=(pltp...  30.1 us
    unnamed x2, local copies, waits for them, and re-layouts  1.15 us

commit v1 on v0

v1 whole, which is shorter than its diff:
```python
import functools

import jax
import jax.numpy as jnp
from jax import lax
from jax.experimental import pallas as pl
from jax.experimental.pallas import tpu as pltpu
from jax.sharding import PartitionSpec as P

MESH = pl.DeviceIdType.MESH
F32 = jnp.float32
BF16 = jnp.bfloat16
ROWS = 16


def kernel(
    nd,
    nl,
    comp,
    own_src_hbm,
    send_block_hbm,
    send_target_hbm,
    send_count_hbm,
    left_block_hbm,
    left_target_hbm,
    left_count_hbm,
    fields_hbm,
    own_hbm,
    send_hbm,
    left_hbm,
    out_ref,
    tot_ref,
    own_src,
    send_block,
    send_target,
    send_count,
    left_block,
    left_target,
    left_count,
    fields,
    own_w,
    send_w,
    left_w,
    load_sem,
    rounded,
    own_acc,
    sbuf,
    rbuf,
    lsbuf,
    lrbuf,
    trow,
    urow,
    go_lvl,
    send_sem,
    recv_sem,
):
    dev = lax.axis_index("dev")
    lvl = lax.axis_index("level")
    blocks, cells = own_w.shape[:2]
    cap = send_w.shape[1]
    lcap = left_w.shape[1]

    tables = [
        (left_block_hbm, left_block),
        (left_count_hbm, left_count),
        (left_target_hbm, left_target),
        (send_block_hbm, send_block),
        (send_count_hbm, send_count),
        (send_target_hbm, send_target),
        (own_src_hbm, own_src),
        (fields_hbm, fields),
    ]
    table_loads = [pltpu.make_async_copy(src, dst, load_sem.at[0]) for src, dst in tables]
    left_load = pltpu.make_async_copy(left_hbm, left_w, load_sem.at[1])
    send_load = pltpu.make_async_copy(send_hbm, send_w, load_sem.at[2])
    own_load = pltpu.make_async_copy(own_hbm, own_w, load_sem.at[3])
    for load in [*table_loads, left_load, send_load, own_load]:
        load.start()

    barrier = pltpu.get_barrier_semaphore()

    def at_dev(p):
        return {"dev": p, "level": lvl}

    def at_lvl(p):
        return {"dev": dev, "level": p}

    def other_devs(step):
        pl.loop(0, dev)(step)
        pl.loop(dev + 1, nd)(step)

    @other_devs
    def _(p):
        pl.semaphore_signal(barrier, inc=1, device_id=at_dev(p), device_id_type=MESH)

    @pl.loop(lvl + 1, nl)
    def _(p):
        pl.semaphore_signal(barrier, inc=1, device_id=at_lvl(p), device_id_type=MESH)

    zero = jnp.zeros((2 * ROWS, cells), BF16)
    rbuf[dev] = zero
    lrbuf[lvl] = zero

    for load in table_loads:
        load.wait()

    pad = jnp.zeros((ROWS - comp, cells), F32)
    for b in range(blocks):
        block = fields[pl.ds(b, comp, stride=blocks), :]
        rounded[b] = jnp.concatenate([block, pad], axis=0).astype(BF16)
    rounded[blocks] = jnp.zeros((ROWS, cells), BF16)

    row_id = lax.broadcasted_iota(jnp.int32, (ROWS, cells), 0)

    def product(index, weight):
        return jnp.dot(rounded[index], weight, preferred_element_type=F32)

    def message(buf, p, c, slot_block, slot_target, slot_count, weights):
        index = jnp.where(c < slot_count[0, p], slot_block[c, p], blocks)
        term = product(index, weights[p, c])
        target = slot_target[c, p].astype(F32)
        buf[p, c * ROWS : (c + 1) * ROWS, :] = jnp.where(row_id == comp, target, term).astype(BF16)
        return term

    part = jnp.zeros((ROWS, cells), F32)
    left_load.wait()
    for p in range(nl):
        for c in range(lcap):
            part += message(lsbuf, p, c, left_block, left_target, left_count, left_w)
    send_load.wait()
    own_load.wait()
    for p in range(nd):
        for c in range(cap):
            part += message(sbuf, p, c, send_block, send_target, send_count, send_w)
    for b in range(blocks):
        term = product(own_src[0, b], own_w[b])
        part += term
        own_acc[b] = term

    sums = jnp.sum(part, axis=1, keepdims=True)
    same = row_id == lax.broadcasted_iota(jnp.int32, (ROWS, cells), 1)
    row = jnp.sum(jnp.where(same, sums, 0.0), axis=0, keepdims=True)
    trow[dev] = row

    def send(src, dst, k, who):
        pltpu.make_async_remote_copy(
            src_ref=src, dst_ref=dst, send_sem=send_sem.at[k], recv_sem=recv_sem.at[k], device_id=who, device_id_type=MESH
        ).start()

    pl.semaphore_wait(barrier, nd - 1 + lvl)

    @other_devs
    def _(p):
        send(trow.at[dev], trow.at[dev], 0, at_dev(p))

    @pl.loop(0, lvl)
    def _(p):
        send(lsbuf.at[p], lrbuf.at[lvl], 1, at_lvl(p))

    @pl.loop(0, lvl)
    def _(p):
        pl.semaphore_signal(go_lvl, inc=1, device_id=at_lvl(p), device_id_type=MESH)

    def wait_recv(buf, n, k):
        ref = buf.at[pl.ds(0, n - 1)]
        pltpu.make_async_copy(ref, ref, recv_sem.at[k]).wait()

    def wait_send(buf, n, k):
        ref = buf.at[pl.ds(0, n - 1)]
        pltpu.make_async_copy(ref, ref, send_sem.at[k]).wait()

    def total(ref, n):
        terms = [ref[i] for i in range(n)]
        while len(terms) > 1:
            half = len(terms) // 2
            terms = [a + b for a, b in zip(terms[:half], terms[half:])] + terms[2 * half :]
        return terms[0]

    wait_recv(trow, nd, 0)
    urow[lvl] = total(trow, nd)

    @pl.loop(0, lvl)
    def _(p):
        send(urow.at[lvl], urow.at[lvl], 3, at_lvl(p))

    def place(buf, acc, p, slots):
        for c in range(slots):
            got = buf[p, c * ROWS : (c + 1) * ROWS, :].astype(F32)
            target = jnp.broadcast_to(got[comp : comp + 1], (ROWS, cells))
            acc = [a + jnp.where(target == float(b), got, 0.0) for b, a in enumerate(acc)]
        return acc

    @other_devs
    def _(p):
        send(sbuf.at[p], rbuf.at[dev], 2, at_dev(p))

    @pl.when(lvl < nl - 1)
    def _():
        pl.semaphore_wait(go_lvl, nl - 1 - lvl)

    @pl.loop(lvl + 1, nl)
    def _(p):
        send(urow.at[lvl], urow.at[lvl], 3, at_lvl(p))

    @pl.loop(lvl + 1, nl)
    def _(p):
        send(lsbuf.at[p], lrbuf.at[lvl], 1, at_lvl(p))

    acc = [own_acc[b] for b in range(blocks)]
    wait_recv(rbuf, nd, 2)
    acc = lax.fori_loop(0, nd, lambda p, a: place(rbuf, a, p, cap), acc)
    wait_recv(lrbuf, nl, 1)
    acc = lax.fori_loop(0, nl, lambda p, a: place(lrbuf, a, p, lcap), acc)
    for b in range(blocks):
        out_ref[pl.ds(b, comp, stride=blocks), :] = acc[b][:comp]
    wait_send(trow, nd, 0)
    wait_send(lsbuf, nl, 1)
    wait_send(sbuf, nd, 2)
    wait_send(urow, nl, 3)
    wait_recv(urow, nl, 3)
    tot_ref[...] = (total(urow, nl) / (cells * blocks))[0, :comp]


def solution(mesh):
    nd = mesh.shape["dev"]
    nl = mesh.shape["level"]

    def body(
        fields,
        own_src,
        own_weight,
        send_block,
        send_target,
        send_count,
        send_weight,
        left_block,
        left_target,
        left_count,
        left_weight,
    ):
        blocks, comp, cells = fields.shape[1:]
        cap = send_weight.shape[3]
        lcap = left_weight.shape[3]
        smem = functools.partial(pltpu.SMEM, dtype=jnp.int32)
        hbm = pl.BlockSpec(memory_space=pl.ANY)
        vmem = pl.BlockSpec(memory_space=pltpu.VMEM)
        dma = pltpu.SemaphoreType.DMA
        remapped, totals = pl.pallas_call(
            functools.partial(kernel, nd, nl, comp),
            out_shape=(
                pltpu.VMEM((comp * blocks, cells), F32),
                pltpu.VMEM((comp,), F32),
            ),
            in_specs=[hbm] * 11,
            out_specs=(vmem, vmem),
            scratch_shapes=[
                smem((1, blocks)),
                smem((cap, nd)),
                smem((cap, nd)),
                smem((1, nd)),
                smem((lcap, nl)),
                smem((lcap, nl)),
                smem((1, nl)),
                pltpu.VMEM((comp * blocks, cells), F32),
                pltpu.VMEM((blocks, cells, cells), BF16),
                pltpu.VMEM((nd, cap, cells, cells), BF16),
                pltpu.VMEM((nl, lcap, cells, cells), BF16),
                dma((4,)),
                pltpu.VMEM((blocks + 1, ROWS, cells), BF16),
                pltpu.VMEM((blocks, ROWS, cells), F32),
                pltpu.VMEM((nd, cap * ROWS, cells), BF16),
                pltpu.VMEM((nd, cap * ROWS, cells), BF16),
                pltpu.VMEM((nl, lcap * ROWS, cells), BF16),
                pltpu.VMEM((nl, lcap * ROWS, cells), BF16),
                pltpu.VMEM((nd, 1, cells), F32),
                pltpu.VMEM((nl, 1, cells), F32),
                pltpu.SemaphoreType.REGULAR,
                dma((4,)),
                dma((4,)),
            ],
            compiler_params=pltpu.CompilerParams(collective_id=0, has_side_effects=True),
        )(
            own_src,
            send_block[0, 0].T,
            send_target[0, 0].T,
            send_count[0],
            left_block[0, 0].T,
            left_target[0, 0].T,
            left_count[0],
            fields[0].transpose(1, 0, 2).reshape(comp * blocks, cells),
            own_weight[0],
            send_weight[0, 0],
            left_weight[0, 0],
        )
        remapped = remapped.reshape(comp, blocks, cells).transpose(1, 0, 2)
        return remapped[None], totals

    in_specs = (
        P("level", "dev", None, None),
        P("level", "dev"),
        P("level", "dev", None, None),
        P("level", "dev", None, None),
        P("level", "dev", None, None),
        P("level", "dev", None),
        P("level", "dev", None, None, None, None),
        P("level", "dev", None, None),
        P("level", "dev", None, None),
        P("level", "dev", None),
        P("level", "dev", None, None, None, None),
    )
    out_specs = (P("level", "dev", None, None), P())
    return jax.shard_map(body, mesh=mesh, in_specs=in_specs, out_specs=out_specs, check_vma=False)
```

time: 32.1 us -> 28.2 us (0.88)
  Pallas kernels: 30.1 us -> 26.3 us
    pallas_call x1, Pallas kernels: 30.1 us -> 26.3 us  [body(): pl.pallas_call(functools.partial(kernel, nd, nl, comp), out_shape=(pltpu....]
where the time goes in v1:
time: 28.2 us; the launch traced here: 28.1 us
  Pallas kernels  26.3 us (93%)
  local copies, waits for them, and re-layouts  1.15 us (4%)
  between operations  0.64 us (2%)
    pallas_call x1, Pallas kernels, body(): pl.pallas_call(functools.partial(kernel, nd, nl, comp), out_shape=(pltpu....  26.3 us
    unnamed x2, local copies, waits for them, and re-layouts  1.15 us

profile of v1, /device:TPU:1, one launch (start us, length us, event | category | flops | bytes accessed | tf_op | source)
XLA Modules:
  0.0 28.1 jit_solution(13524426416224007521)
XLA Ops:
  0.6 26.3 %shard_map.122 = (f32[192,128]{1,0:T(8,128)S(1)}, f32[12]{0:T(128)S(1)}) custom-call(s32[1,16]{1,0:T(1,128)} %own_src_hbm.1, s32[2,32]{1,0:T(2,128)} %bitcast.32, s32[2,32]{1,0:T(2,128)} %bitcast.33, s32[1,32]{1,0:T(1,128)} %bitcast.36, s32[2,16]{1,0:T(2,128)} %bitcast.34, s32[2,16]{1,0:T(2,128)} %bitcast.35, s32[1,16]{1,0:T(1,128)} %bitcast.37, ...), custom_call_target="tpu_custom_call" | custom-call | tf_op jit(solution)/shard_map/pallas_call | solution.py:248
  26.9 0.6 %copy.15 = f32[1,16,12,128]{3,1,2,0:T(8,128)} copy(f32[1,16,12,128]{3,1,2,0:T(8,128)S(1)} %bitcast.27) | data formatting | bytes 196608
  27.6 0.5 %copy.16 = f32[12]{0:T(128)} copy(f32[12]{0:T(128)S(1)} %get-tuple-element.7) | data formatting | bytes 96

commit v2 on v1

--- a/solution.py
+++ b/solution.py
@@ -11,6 +11,7 @@
 F32 = jnp.float32
 BF16 = jnp.bfloat16
 ROWS = 16
+PIECES = 4
 
 
 def kernel(
@@ -71,10 +72,22 @@
         (fields_hbm, fields),
     ]
     table_loads = [pltpu.make_async_copy(src, dst, load_sem.at[0]) for src, dst in tables]
-    left_load = pltpu.make_async_copy(left_hbm, left_w, load_sem.at[1])
-    send_load = pltpu.make_async_copy(send_hbm, send_w, load_sem.at[2])
-    own_load = pltpu.make_async_copy(own_hbm, own_w, load_sem.at[3])
-    for load in [*table_loads, left_load, send_load, own_load]:
+    half = nd // 2
+
+    def pieces(src, dst, lo, hi, n, k):
+        size = (hi - lo) // n
+        return [
+            pltpu.make_async_copy(
+                src.at[lo + i * size : lo + (i + 1) * size], dst.at[lo + i * size : lo + (i + 1) * size], load_sem.at[k]
+            )
+            for i in range(n)
+        ]
+
+    left_load = pieces(left_hbm, left_w, 0, nl, PIECES, 1)
+    first_load = pieces(send_hbm, send_w, 0, half, PIECES, 2)
+    second_load = pieces(send_hbm, send_w, half, nd, PIECES, 3)
+    own_load = pieces(own_hbm, own_w, 0, blocks, PIECES // 2, 4)
+    for load in [*table_loads, *left_load, *first_load, *second_load, *own_load]:
         load.start()
 
     barrier = pltpu.get_barrier_semaphore()
@@ -93,9 +106,21 @@
     def _(p):
         pl.semaphore_signal(barrier, inc=1, device_id=at_dev(p), device_id_type=MESH)
 
+    summing = dev % 2 == 1
+    partner = dev + 1 - 2 * (dev % 2)
+
+    def at_partner(p):
+        return {"dev": partner, "level": p}
+
     @pl.loop(lvl + 1, nl)
     def _(p):
         pl.semaphore_signal(barrier, inc=1, device_id=at_lvl(p), device_id_type=MESH)
+
+    @pl.when(jnp.logical_not(summing))
+    def _():
+        @pl.loop(lvl + 1, nl)
+        def _(p):
+            pl.semaphore_signal(barrier, inc=1, device_id=at_partner(p), device_id_type=MESH)
 
     zero = jnp.zeros((2 * ROWS, cells), BF16)
     rbuf[dev] = zero
@@ -123,13 +148,21 @@
         return term
 
     part = jnp.zeros((ROWS, cells), F32)
-    left_load.wait()
+    for load in left_load:
+        load.wait()
     for p in range(nl):
         for c in range(lcap):
             part += message(lsbuf, p, c, left_block, left_target, left_count, left_w)
-    send_load.wait()
-    own_load.wait()
-    for p in range(nd):
+    for load in first_load:
+        load.wait()
+    for p in range(half):
+        for c in range(cap):
+            part += message(sbuf, p, c, send_block, send_target, send_count, send_w)
+    for load in second_load:
+        load.wait()
+    for load in own_load:
+        load.wait()
+    for p in range(half, nd):
         for c in range(cap):
             part += message(sbuf, p, c, send_block, send_target, send_count, send_w)
     for b in range(blocks):
@@ -147,19 +180,21 @@
             src_ref=src, dst_ref=dst, send_sem=send_sem.at[k], recv_sem=recv_sem.at[k], device_id=who, device_id_type=MESH
         ).start()
 
-    pl.semaphore_wait(barrier, nd - 1 + lvl)
-
-    @other_devs
-    def _(p):
-        send(trow.at[dev], trow.at[dev], 0, at_dev(p))
+    pl.semaphore_wait(barrier, nd - 1 + lvl + lvl * (dev % 2))
 
     @pl.loop(0, lvl)
     def _(p):
+        pl.semaphore_signal(go_lvl, inc=1, device_id=at_lvl(p), device_id_type=MESH)
+
+    def report(i):
+        send(trow.at[dev], trow.at[dev], 0, at_dev(2 * i + 1))
+
+    pl.loop(0, dev // 2)(report)
+    pl.loop((dev + 1) // 2, nd // 2)(report)
+
+    @pl.loop(0, lvl)
+    def _(p):
         send(lsbuf.at[p], lrbuf.at[lvl], 1, at_lvl(p))
-
-    @pl.loop(0, lvl)
-    def _(p):
-        pl.semaphore_signal(go_lvl, inc=1, device_id=at_lvl(p), device_id_type=MESH)
 
     def wait_recv(buf, n, k):
         ref = buf.at[pl.ds(0, n - 1)]
@@ -176,12 +211,16 @@
             terms = [a + b for a, b in zip(terms[:half], terms[half:])] + terms[2 * half :]
         return terms[0]
 
-    wait_recv(trow, nd, 0)
-    urow[lvl] = total(trow, nd)
-
-    @pl.loop(0, lvl)
-    def _(p):
+    def tell(p):
         send(urow.at[lvl], urow.at[lvl], 3, at_lvl(p))
+        send(urow.at[lvl], urow.at[lvl], 3, at_partner(p))
+
+    @pl.when(summing)
+    def _():
+        wait_recv(trow, nd, 0)
+        urow[lvl] = total(trow, nd)
+        pl.loop(0, lvl)(tell)
+        send(urow.at[lvl], urow.at[lvl], 3, at_partner(lvl))
 
     def place(buf, acc, p, slots):
         for c in range(slots):
@@ -200,11 +239,11 @@
 
     @pl.loop(lvl + 1, nl)
     def _(p):
-        send(urow.at[lvl], urow.at[lvl], 3, at_lvl(p))
-
-    @pl.loop(lvl + 1, nl)
-    def _(p):
         send(lsbuf.at[p], lrbuf.at[lvl], 1, at_lvl(p))
+
+    @pl.when(summing)
+    def _():
+        pl.loop(lvl + 1, nl)(tell)
 
     acc = [own_acc[b] for b in range(blocks)]
     wait_recv(rbuf, nd, 2)
@@ -213,12 +252,32 @@
     acc = lax.fori_loop(0, nl, lambda p, a: place(lrbuf, a, p, lcap), acc)
     for b in range(blocks):
         out_ref[pl.ds(b, comp, stride=blocks), :] = acc[b][:comp]
-    wait_send(trow, nd, 0)
     wait_send(lsbuf, nl, 1)
     wait_send(sbuf, nd, 2)
-    wait_send(urow, nl, 3)
-    wait_recv(urow, nl, 3)
+
+    @pl.when(summing)
+    def _():
+        wait_send(trow, nd // 2, 0)
+        wait_send(trow, 2 * nl, 3)
+        wait_recv(urow, nl, 3)
+
+    @pl.when(jnp.logical_not(summing))
+    def _():
+        wait_send(trow, nd // 2 + 1, 0)
+        wait_recv(urow, nl + 1, 3)
+
     tot_ref[...] = (total(urow, nl) / (cells * blocks))[0, :comp]
+
+
+def deliver(blocks_in, totals_in, blocks_out, totals_out, sem):
+    copies = [
+        pltpu.make_async_copy(blocks_in, blocks_out, sem.at[0]),
+        pltpu.make_async_copy(totals_in, totals_out, sem.at[1]),
+    ]
+    for copy in copies:
+        copy.start()
+    for copy in copies:
+        copy.wait()
 
 
 def solution(mesh):
@@ -265,7 +324,7 @@
                 pltpu.VMEM((blocks, cells, cells), BF16),
                 pltpu.VMEM((nd, cap, cells, cells), BF16),
                 pltpu.VMEM((nl, lcap, cells, cells), BF16),
-                dma((4,)),
+                dma((5,)),
                 pltpu.VMEM((blocks + 1, ROWS, cells), BF16),
                 pltpu.VMEM((blocks, ROWS, cells), F32),
                 pltpu.VMEM((nd, cap * ROWS, cells), BF16),
@@ -292,6 +351,17 @@
             send_weight[0, 0],
             left_weight[0, 0],
         )
+        remapped, totals = pl.pallas_call(
+            deliver,
+            out_shape=(
+                jax.ShapeDtypeStruct((comp * blocks, cells), F32),
+                jax.ShapeDtypeStruct((comp,), F32),
+            ),
+            in_specs=[vmem] * 2,
+            out_specs=(hbm, hbm),
+            scratch_shapes=[dma((2,))],
+            compiler_params=pltpu.CompilerParams(vmem_limit_bytes=1 << 20),
+        )(pltpu.with_memory_space_constraint(remapped, pltpu.VMEM), pltpu.with_memory_space_constraint(totals, pltpu.VMEM))
         remapped = remapped.reshape(comp, blocks, cells).transpose(1, 0, 2)
         return remapped[None], totals
 

time: 28.2 us -> 27.5 us (0.975)
  local copies, waits for them, and re-layouts: 1.15 us -> 0 us
  Pallas kernels: 26.3 us -> 26.7 us
    unnamed x2 -> x0, local copies, waits for them, and re-layouts: 1.15 us -> none
    pallas_call x0 -> x1, Pallas kernels: none -> 0.66 us  [body(): pl.pallas_call(deliver, out_shape=(jax.ShapeDtypeStruct((comp * blocks, c...]
where the time goes in v2:
time: 27.5 us; the launch traced here: 27.4 us
  Pallas kernels  26.7 us (97%)
  between operations  0.64 us (2%)
    pallas_call x1, Pallas kernels, body(): pl.pallas_call(functools.partial(kernel, nd, nl, comp), out_shape=(pltpu....  26.1 us
    pallas_call x1, Pallas kernels, body(): pl.pallas_call(deliver, out_shape=(jax.ShapeDtypeStruct((comp * blocks, c...  0.66 us

profile of v2, /device:TPU:1, one launch (start us, length us, event | category | flops | bytes accessed | tf_op | source)
XLA Modules:
  0.0 27.4 jit_solution(7296223903091423266)
XLA Ops:
  0.6 26.1 %shard_map.122 = (f32[192,128]{1,0:T(8,128)S(1)}, f32[12]{0:T(128)S(1)}) custom-call(s32[1,16]{1,0:T(1,128)} %own_src_hbm.1, s32[2,32]{1,0:T(2,128)} %bitcast.31, s32[2,32]{1,0:T(2,128)} %bitcast.32, s32[1,32]{1,0:T(1,128)} %bitcast.35, s32[2,16]{1,0:T(2,128)} %bitcast.33, s32[2,16]{1,0:T(2,128)} %bitcast.34, s32[1,16]{1,0:T(1,128)} %bitcast.36, ...), custom_call_target="tpu_custom_call" | custom-call | tf_op jit(solution)/shard_map/pallas_call | solution.py:307
  26.7 0.7 %shard_map.123 = (f32[192,128]{1,0:T(8,128)}, f32[12]{0:T(128)}) custom-call(f32[192,128]{1,0:T(8,128)S(1)} %get-tuple-element.6.blocks_in, f32[12]{0:T(128)S(1)} %get-tuple-element.7.totals_in), custom_call_target="tpu_custom_call" | custom-call | tf_op jit(solution)/shard_map/pallas_call | solution.py:354

commit v3 on v2

--- a/solution.py
+++ b/solution.py
@@ -11,6 +11,8 @@
 F32 = jnp.float32
 BF16 = jnp.bfloat16
 ROWS = 16
+HALF = 8
+PACKED = 24
 PIECES = 4
 
 
@@ -36,7 +38,6 @@
     send_target,
     send_count,
     left_block,
-    left_target,
     left_count,
     fields,
     own_w,
@@ -51,6 +52,9 @@
     lrbuf,
     trow,
     urow,
+    every,
+    places,
+    targets,
     go_lvl,
     send_sem,
     recv_sem,
@@ -64,12 +68,12 @@
     tables = [
         (left_block_hbm, left_block),
         (left_count_hbm, left_count),
-        (left_target_hbm, left_target),
         (send_block_hbm, send_block),
         (send_count_hbm, send_count),
         (send_target_hbm, send_target),
         (own_src_hbm, own_src),
         (fields_hbm, fields),
+        (left_target_hbm, places.at[lvl]),
     ]
     table_loads = [pltpu.make_async_copy(src, dst, load_sem.at[0]) for src, dst in tables]
     half = nd // 2
@@ -122,9 +126,23 @@
         def _(p):
             pl.semaphore_signal(barrier, inc=1, device_id=at_partner(p), device_id_type=MESH)
 
+    first_dev, first_lvl = 1, 0
+    is_first = jnp.logical_and(dev == first_dev, lvl == first_lvl)
+    is_far = jnp.logical_and(dev != first_dev, lvl != first_lvl)
+
+    @pl.when(is_first)
+    def _():
+        @pl.loop(1, nl)
+        def _(l):
+            def greet(p):
+                pl.semaphore_signal(barrier, inc=1, device_id={"dev": p, "level": l}, device_id_type=MESH)
+
+            pl.loop(0, first_dev)(greet)
+            pl.loop(first_dev + 1, nd)(greet)
+
     zero = jnp.zeros((2 * ROWS, cells), BF16)
     rbuf[dev] = zero
-    lrbuf[lvl] = zero
+    lrbuf[lvl, :PACKED] = zero[:PACKED]
 
     for load in table_loads:
         load.wait()
@@ -151,8 +169,13 @@
     for load in left_load:
         load.wait()
     for p in range(nl):
-        for c in range(lcap):
-            part += message(lsbuf, p, c, left_block, left_target, left_count, left_w)
+        terms = [
+            product(jnp.where(c < left_count[0, p], left_block[c, p], blocks), left_w[p, c]) for c in range(lcap)
+        ]
+        part += terms[0] + terms[1]
+        middle = terms[0][HALF:] + pltpu.roll(terms[1][HALF:], HALF // 2, 0)
+        packed = jnp.concatenate([terms[0][:HALF], middle, terms[1][:HALF]], axis=0)
+        lsbuf[p, :PACKED] = packed.astype(BF16)
     for load in first_load:
         load.wait()
     for p in range(half):
@@ -180,7 +203,7 @@
             src_ref=src, dst_ref=dst, send_sem=send_sem.at[k], recv_sem=recv_sem.at[k], device_id=who, device_id_type=MESH
         ).start()
 
-    pl.semaphore_wait(barrier, nd - 1 + lvl + lvl * (dev % 2))
+    pl.semaphore_wait(barrier, nd - 1 + lvl + lvl * (dev % 2) + jnp.where(is_far, 1, 0))
 
     @pl.loop(0, lvl)
     def _(p):
@@ -189,12 +212,18 @@
     def report(i):
         send(trow.at[dev], trow.at[dev], 0, at_dev(2 * i + 1))
 
+    @pl.when(lvl != first_lvl)
+    def _():
+        send(trow.at[dev], every.at[lvl, dev], 4, {"dev": first_dev, "level": first_lvl})
+
     pl.loop(0, dev // 2)(report)
     pl.loop((dev + 1) // 2, nd // 2)(report)
 
-    @pl.loop(0, lvl)
-    def _(p):
-        send(lsbuf.at[p], lrbuf.at[lvl], 1, at_lvl(p))
+    def pass_on(p):
+        send(lsbuf.at[p, :PACKED], lrbuf.at[lvl, :PACKED], 1, at_lvl(p))
+        send(places.at[lvl], places.at[lvl], 5, at_lvl(p))
+
+    pl.loop(0, lvl)(pass_on)
 
     def wait_recv(buf, n, k):
         ref = buf.at[pl.ds(0, n - 1)]
@@ -219,7 +248,12 @@
     def _():
         wait_recv(trow, nd, 0)
         urow[lvl] = total(trow, nd)
-        pl.loop(0, lvl)(tell)
+        pl.loop(jnp.where(dev == first_dev, jnp.minimum(1, lvl), 0), lvl)(tell)
+
+        @pl.when(jnp.logical_and(dev == first_dev, lvl > 0))
+        def _():
+            send(urow.at[lvl], urow.at[lvl], 3, at_partner(0))
+
         send(urow.at[lvl], urow.at[lvl], 3, at_partner(lvl))
 
     def place(buf, acc, p, slots):
@@ -237,9 +271,7 @@
     def _():
         pl.semaphore_wait(go_lvl, nl - 1 - lvl)
 
-    @pl.loop(lvl + 1, nl)
-    def _(p):
-        send(lsbuf.at[p], lrbuf.at[lvl], 1, at_lvl(p))
+    pl.loop(lvl + 1, nl)(pass_on)
 
     @pl.when(summing)
     def _():
@@ -248,25 +280,79 @@
     acc = [own_acc[b] for b in range(blocks)]
     wait_recv(rbuf, nd, 2)
     acc = lax.fori_loop(0, nd, lambda p, a: place(rbuf, a, p, cap), acc)
-    wait_recv(lrbuf, nl, 1)
-    acc = lax.fori_loop(0, nl, lambda p, a: place(lrbuf, a, p, lcap), acc)
+    wait_recv(lrbuf.at[:, :PACKED], nl, 1)
+    wait_recv(places, nl, 5)
+    at_level = lax.broadcasted_iota(jnp.int32, (lcap, nl), 1) == lvl
+    for p in range(nl):
+        target = jnp.sum(jnp.where(at_level, places[p].astype(F32), 0.0), axis=1, keepdims=True)
+        targets[p] = jnp.broadcast_to(target, (lcap, cells))
+    low = lax.broadcasted_iota(jnp.int32, (HALF, cells), 0) < HALF // 2
+    heads = [a[:HALF] for a in acc]
+    tails = [jnp.where(low, a[HALF:], 0.0) for a in acc]
+
+    def unpack(p, state):
+        heads, tails = state
+        got = lrbuf[p, :PACKED].astype(F32)
+        first, middle, second = got[:HALF], got[HALF : 2 * HALF], got[2 * HALF :]
+        to_first = jnp.broadcast_to(targets[p, 0:1], (HALF, cells))
+        to_second = jnp.broadcast_to(targets[p, 1:2], (HALF, cells))
+        to_middle = jnp.where(low, to_first, to_second)
+        heads = [
+            h + jnp.where(to_first == float(b), first, 0.0) + jnp.where(to_second == float(b), second, 0.0)
+            for b, h in enumerate(heads)
+        ]
+        tails = [t + jnp.where(to_middle == float(b), middle, 0.0) for b, t in enumerate(tails)]
+        return heads, tails
+
+    heads, tails = lax.fori_loop(0, nl, unpack, (heads, tails))
     for b in range(blocks):
-        out_ref[pl.ds(b, comp, stride=blocks), :] = acc[b][:comp]
-    wait_send(lsbuf, nl, 1)
+        tail = tails[b] + pltpu.roll(tails[b], HALF // 2, 0)
+        out_ref[pl.ds(b, comp, stride=blocks), :] = jnp.concatenate([heads[b], tail], axis=0)[:comp]
+    wait_send(lsbuf.at[:, :PACKED], nl, 1)
+    wait_send(places, nl, 5)
     wait_send(sbuf, nd, 2)
 
-    @pl.when(summing)
+    def finish(rows):
+        tot_ref[...] = (rows / (cells * blocks))[0, :comp]
+
+    @pl.when(lvl != first_lvl)
+    def _():
+        wait_send(trow, 2, 4)
+
+    @pl.when(jnp.logical_and(summing, jnp.logical_not(is_first)))
+    def _():
+        wait_send(trow, nd // 2, 0)
+
+        @pl.when(dev == first_dev)
+        def _():
+            wait_send(trow, 2 * nl - 1, 3)
+
+        @pl.when(dev != first_dev)
+        def _():
+            wait_send(trow, 2 * nl, 3)
+
+        wait_recv(urow, nl, 3)
+        finish(total(urow, nl))
+
+    @pl.when(is_first)
     def _():
         wait_send(trow, nd // 2, 0)
         wait_send(trow, 2 * nl, 3)
-        wait_recv(urow, nl, 3)
+        ref = every.at[pl.ds(1, nl - 1)]
+        pltpu.make_async_copy(ref, ref, recv_sem.at[4]).wait()
+        sums = [urow[0]]
+        for l in range(1, nl):
+            sums.append(total(every.at[l], nd))
+        while len(sums) > 1:
+            half = len(sums) // 2
+            sums = [a + b for a, b in zip(sums[:half], sums[half:])] + sums[2 * half :]
+        finish(sums[0])
 
     @pl.when(jnp.logical_not(summing))
     def _():
         wait_send(trow, nd // 2 + 1, 0)
         wait_recv(urow, nl + 1, 3)
-
-    tot_ref[...] = (total(urow, nl) / (cells * blocks))[0, :comp]
+        finish(total(urow, nl))
 
 
 def deliver(blocks_in, totals_in, blocks_out, totals_out, sem):
@@ -318,7 +404,6 @@
                 smem((cap, nd)),
                 smem((1, nd)),
                 smem((lcap, nl)),
-                smem((lcap, nl)),
                 smem((1, nl)),
                 pltpu.VMEM((comp * blocks, cells), F32),
                 pltpu.VMEM((blocks, cells, cells), BF16),
@@ -333,9 +418,12 @@
                 pltpu.VMEM((nl, lcap * ROWS, cells), BF16),
                 pltpu.VMEM((nd, 1, cells), F32),
                 pltpu.VMEM((nl, 1, cells), F32),
+                pltpu.VMEM((nl, nd, 1, cells), F32),
+                pltpu.VMEM((nl, lcap, nl), jnp.int32),
+                pltpu.VMEM((nl, lcap, cells), F32),
                 pltpu.SemaphoreType.REGULAR,
-                dma((4,)),
-                dma((4,)),
+                dma((6,)),
+                dma((6,)),
             ],
             compiler_params=pltpu.CompilerParams(collective_id=0, has_side_effects=True),
         )(

time: 27.5 us -> 26.6 us (0.967)
  Pallas kernels: 26.7 us -> 25.8 us
    pallas_call x1, Pallas kernels: 26.1 us -> 25.1 us  [body(): pl.pallas_call(functools.partial(kernel, nd, nl, comp), out_shape=(pltpu....]
where the time goes in v3:
time: 26.6 us; the launch traced here: 26.4 us
  Pallas kernels  25.8 us (97%)
  between operations  0.64 us (2%)
    pallas_call x1, Pallas kernels, body(): pl.pallas_call(functools.partial(kernel, nd, nl, comp), out_shape=(pltpu....  25.1 us
    pallas_call x1, Pallas kernels, body(): pl.pallas_call(deliver, out_shape=(jax.ShapeDtypeStruct((comp * blocks, c...  0.66 us

profile of v3, /device:TPU:1, one launch (start us, length us, event | category | flops | bytes accessed | tf_op | source)
XLA Modules:
  0.0 26.4 jit_solution(3570823224033877233)
XLA Ops:
  0.6 25.1 %shard_map.122 = (f32[192,128]{1,0:T(8,128)S(1)}, f32[12]{0:T(128)S(1)}) custom-call(s32[1,16]{1,0:T(1,128)} %own_src_hbm.1, s32[2,32]{1,0:T(2,128)} %bitcast.31, s32[2,32]{1,0:T(2,128)} %bitcast.32, s32[1,32]{1,0:T(1,128)} %bitcast.35, s32[2,16]{1,0:T(2,128)} %bitcast.33, s32[2,16]{1,0:T(2,128)} %bitcast.34, s32[1,16]{1,0:T(1,128)} %bitcast.36, ...), custom_call_target="tpu_custom_call" | custom-call | tf_op jit(solution)/shard_map/pallas_call | solution.py:393
  25.8 0.7 %shard_map.123 = (f32[192,128]{1,0:T(8,128)}, f32[12]{0:T(128)}) custom-call(f32[192,128]{1,0:T(8,128)S(1)} %get-tuple-element.6.blocks_in, f32[12]{0:T(128)S(1)} %get-tuple-element.7.totals_in), custom_call_target="tpu_custom_call" | custom-call | tf_op jit(solution)/shard_map/pallas_call | solution.py:442

commit v4 on v3

--- a/solution.py
+++ b/solution.py
@@ -90,7 +90,7 @@
     left_load = pieces(left_hbm, left_w, 0, nl, PIECES, 1)
     first_load = pieces(send_hbm, send_w, 0, half, PIECES, 2)
     second_load = pieces(send_hbm, send_w, half, nd, PIECES, 3)
-    own_load = pieces(own_hbm, own_w, 0, blocks, PIECES // 2, 4)
+    own_load = pieces(own_hbm, own_w, 0, blocks, PIECES // 2, 3)
     for load in [*table_loads, *left_load, *first_load, *second_load, *own_load]:
         load.start()
 
@@ -200,10 +200,14 @@
 
     def send(src, dst, k, who):
         pltpu.make_async_remote_copy(
-            src_ref=src, dst_ref=dst, send_sem=send_sem.at[k], recv_sem=recv_sem.at[k], device_id=who, device_id_type=MESH
+            src_ref=src, dst_ref=dst, send_sem=send_sem, recv_sem=recv_sem.at[k], device_id=who, device_id_type=MESH
         ).start()
 
     pl.semaphore_wait(barrier, nd - 1 + lvl + lvl * (dev % 2) + jnp.where(is_far, 1, 0))
+
+    @pl.when(lvl != first_lvl)
+    def _():
+        send(trow.at[dev], every.at[lvl, dev], 4, {"dev": first_dev, "level": first_lvl})
 
     @pl.loop(0, lvl)
     def _(p):
@@ -212,10 +216,6 @@
     def report(i):
         send(trow.at[dev], trow.at[dev], 0, at_dev(2 * i + 1))
 
-    @pl.when(lvl != first_lvl)
-    def _():
-        send(trow.at[dev], every.at[lvl, dev], 4, {"dev": first_dev, "level": first_lvl})
-
     pl.loop(0, dev // 2)(report)
     pl.loop((dev + 1) // 2, nd // 2)(report)
 
@@ -229,9 +229,9 @@
         ref = buf.at[pl.ds(0, n - 1)]
         pltpu.make_async_copy(ref, ref, recv_sem.at[k]).wait()
 
-    def wait_send(buf, n, k):
+    def wait_send(buf, n):
         ref = buf.at[pl.ds(0, n - 1)]
-        pltpu.make_async_copy(ref, ref, send_sem.at[k]).wait()
+        pltpu.make_async_copy(ref, ref, send_sem).wait()
 
     def total(ref, n):
         terms = [ref[i] for i in range(n)]
@@ -271,7 +271,11 @@
     def _():
         pl.semaphore_wait(go_lvl, nl - 1 - lvl)
 
-    pl.loop(lvl + 1, nl)(pass_on)
+    middle = jnp.minimum(lvl + nl // 2, nl - 1)
+
+    @pl.loop(lvl + 1, nl)
+    def _(q):
+        pass_on(jnp.where(q <= middle, middle + lvl + 1 - q, q))
 
     @pl.when(summing)
     def _():
@@ -308,36 +312,36 @@
     for b in range(blocks):
         tail = tails[b] + pltpu.roll(tails[b], HALF // 2, 0)
         out_ref[pl.ds(b, comp, stride=blocks), :] = jnp.concatenate([heads[b], tail], axis=0)[:comp]
-    wait_send(lsbuf.at[:, :PACKED], nl, 1)
-    wait_send(places, nl, 5)
-    wait_send(sbuf, nd, 2)
+    wait_send(lsbuf.at[:, :PACKED], nl)
+    wait_send(places, nl)
+    wait_send(sbuf, nd)
 
     def finish(rows):
         tot_ref[...] = (rows / (cells * blocks))[0, :comp]
 
     @pl.when(lvl != first_lvl)
     def _():
-        wait_send(trow, 2, 4)
+        wait_send(trow, 2)
 
     @pl.when(jnp.logical_and(summing, jnp.logical_not(is_first)))
     def _():
-        wait_send(trow, nd // 2, 0)
+        wait_send(trow, nd // 2)
 
         @pl.when(dev == first_dev)
         def _():
-            wait_send(trow, 2 * nl - 1, 3)
+            wait_send(trow, 2 * nl - 1)
 
         @pl.when(dev != first_dev)
         def _():
-            wait_send(trow, 2 * nl, 3)
+            wait_send(trow, 2 * nl)
 
         wait_recv(urow, nl, 3)
         finish(total(urow, nl))
 
     @pl.when(is_first)
     def _():
-        wait_send(trow, nd // 2, 0)
-        wait_send(trow, 2 * nl, 3)
+        wait_send(trow, nd // 2)
+        wait_send(trow, 2 * nl)
         ref = every.at[pl.ds(1, nl - 1)]
         pltpu.make_async_copy(ref, ref, recv_sem.at[4]).wait()
         sums = [urow[0]]
@@ -350,7 +354,7 @@
 
     @pl.when(jnp.logical_not(summing))
     def _():
-        wait_send(trow, nd // 2 + 1, 0)
+        wait_send(trow, nd // 2 + 1)
         wait_recv(urow, nl + 1, 3)
         finish(total(urow, nl))
 
@@ -409,7 +413,7 @@
                 pltpu.VMEM((blocks, cells, cells), BF16),
                 pltpu.VMEM((nd, cap, cells, cells), BF16),
                 pltpu.VMEM((nl, lcap, cells, cells), BF16),
-                dma((5,)),
+                dma((4,)),
                 pltpu.VMEM((blocks + 1, ROWS, cells), BF16),
                 pltpu.VMEM((blocks, ROWS, cells), F32),
                 pltpu.VMEM((nd, cap * ROWS, cells), BF16),
@@ -422,7 +426,7 @@
                 pltpu.VMEM((nl, lcap, nl), jnp.int32),
                 pltpu.VMEM((nl, lcap, cells), F32),
                 pltpu.SemaphoreType.REGULAR,
-                dma((6,)),
+                pltpu.SemaphoreType.DMA,
                 dma((6,)),
             ],
             compiler_params=pltpu.CompilerParams(collective_id=0, has_side_effects=True),

time: 26.6 us -> 26.5 us (level)
  no operation moved by 1% of the time
where the time goes in v4:
time: 26.5 us; the launch traced here: 26.4 us
  Pallas kernels  25.7 us (97%)
  between operations  0.64 us (2%)
    pallas_call x1, Pallas kernels, body(): pl.pallas_call(functools.partial(kernel, nd, nl, comp), out_shape=(pltpu....  25.1 us
    pallas_call x1, Pallas kernels, body(): pl.pallas_call(deliver, out_shape=(jax.ShapeDtypeStruct((comp * blocks, c...  0.66 us

profile of v4, /device:TPU:1, one launch (start us, length us, event | category | flops | bytes accessed | tf_op | source)
XLA Modules:
  0.0 26.4 jit_solution(5243810901017656574)
XLA Ops:
  0.6 25.1 %shard_map.122 = (f32[192,128]{1,0:T(8,128)S(1)}, f32[12]{0:T(128)S(1)}) custom-call(s32[1,16]{1,0:T(1,128)} %own_src_hbm.1, s32[2,32]{1,0:T(2,128)} %bitcast.31, s32[2,32]{1,0:T(2,128)} %bitcast.32, s32[1,32]{1,0:T(1,128)} %bitcast.35, s32[2,16]{1,0:T(2,128)} %bitcast.33, s32[2,16]{1,0:T(2,128)} %bitcast.34, s32[1,16]{1,0:T(1,128)} %bitcast.36, ...), custom_call_target="tpu_custom_call" | custom-call | tf_op jit(solution)/shard_map/pallas_call | solution.py:397
  25.7 0.7 %shard_map.123 = (f32[192,128]{1,0:T(8,128)}, f32[12]{0:T(128)}) custom-call(f32[192,128]{1,0:T(8,128)S(1)} %get-tuple-element.6.blocks_in, f32[12]{0:T(128)S(1)} %get-tuple-element.7.totals_in), custom_call_target="tpu_custom_call" | custom-call | tf_op jit(solution)/shard_map/pallas_call | solution.py:446
